TPU v7x, 8 devices: a whole 2x2x1 slice. The times are simulated.
8 devices in a mesh: dp: 1 (over z), tp: 2 (over y), ep: 4 (over x, core).
Axes of the slice: x: 2, y: 2, z: 1, core: 2. Of those that a mesh axis runs over, the one named last changes fastest.
Arguments:
- x: bfloat16 [4096, 2048], P(('dp', 'ep', 'tp'))
- idx: int32 [4096, 8], P(('dp', 'ep', 'tp'))
- gate: float32 [4096, 8], P(('dp', 'ep', 'tp'))
- w1: bfloat16 [64, 2048, 1024], P('ep', None, 'tp')
- w3: bfloat16 [64, 2048, 1024], P('ep', None, 'tp')
- w2: bfloat16 [64, 1024, 2048], P('ep', 'tp')
Outputs:
- output: bfloat16 [4096, 2048], P(('dp', 'ep', 'tp'))
All inputs are finite; a program needn't handle non-finite values.
Results may differ from a plain program's by a relative error of at most 0.001.
Values are sent between devices in bfloat16 or wider.
A program may use at most 1 GiB of HBM per device.

v0:
```python
import jax
import jax.numpy as jnp
from jax import lax
from jax.sharding import PartitionSpec as P


def _groups(idx, gate, lo, n_exp, cap):
    k = idx.shape[1]
    flat = idx.reshape(-1) - lo
    key = jnp.where((flat >= 0) & (flat < n_exp), flat, n_exp)
    order = jnp.argsort(key)
    counts = jnp.zeros((n_exp + 1,), jnp.int32).at[key].add(1)[:n_exp]
    starts = jnp.cumsum(counts) - counts
    slot = jnp.arange(cap)
    pid = order[jnp.clip(starts[:, None] + slot[None, :], 0, flat.shape[0] - 1)]
    g = jnp.where(slot[None, :] < counts[:, None], gate.reshape(-1)[pid], 0.0)
    return pid // k, g


def _experts(x, tok, g, w1, w3, w2):
    xg = x[tok]
    a = jnp.einsum('ecd,edf->ecf', xg, w1, preferred_element_type=jnp.float32)
    b = jnp.einsum('ecd,edf->ecf', xg, w3, preferred_element_type=jnp.float32)
    h = (jax.nn.silu(a) * b).astype(jnp.bfloat16)
    o = jnp.einsum('ecf,efd->ecd', h, w2, preferred_element_type=jnp.float32) * g[..., None]
    d = x.shape[1]
    return jnp.zeros(x.shape, jnp.float32).at[tok.reshape(-1)].add(o.reshape(-1, d))


def solution(mesh):
    n_pos = mesh.shape['ep']
    rows_spec = P(('dp', 'ep', 'tp'), None)

    def body(x, idx, gate, w1, w3, w2):
        xa = lax.all_gather(x, ('ep', 'tp'), axis=0, tiled=True)
        ia = lax.all_gather(idx, ('ep', 'tp'), axis=0, tiled=True)
        ga = lax.all_gather(gate, ('ep', 'tp'), axis=0, tiled=True)
        rows = xa.shape[0]
        n_exp, k = w1.shape[0], idx.shape[1]
        cap = 8 * ((k * rows // (n_exp * n_pos) + 9) // 8)
        lo = lax.axis_index('ep') * n_exp
        tok, g = _groups(ia, ga, lo, n_exp, cap)
        part = _experts(xa, tok, g, w1, w3, w2)
        y = lax.psum_scatter(part, ('ep', 'tp'), scatter_dimension=0, tiled=True)
        return y.astype(jnp.bfloat16)

    return jax.shard_map(body, mesh=mesh,
                         in_specs=(rows_spec, rows_spec, rows_spec,
                                   P('ep', None, 'tp'), P('ep', None, 'tp'), P('ep', 'tp', None)),
                         out_specs=rows_spec, check_vma=False)
```

profile of v0, /device:TPU:0, one launch (start us, length us, event | category | flops | bytes accessed | tf_op | source)
XLA Modules:
  0.0 861.4 jit_solution(9264084116147243880)
XLA Ops:
  6.5 0.0 copy-start
  6.5 0.0 all-gather.2.cloned.1.call-start
  6.5 0.7 all-gather.2.cloned.1.call-update
  7.3 0.0 reduce-scatter.2.cloned.1.call-start
  7.3 14.0 %all_gather.9 = s32[4096,8]{0,1:T(8,128)S(1)} all-gather(s32[512,8]{0,1:T(8,128)} %param.7), channel_id=1, replica_groups=mesh['dp'=1,'tp'=2,'ep'=4] {'ep','tp'}, dimensions={0}, use_global_device_ids=true | all-gather | bytes 147456 | tf_op jit(solution)/shard_map/all_gather | solution.py:36
  21.4 0.6 copy.8
  22.0 1.1 sub.33
  23.0 1.0 sub.32
  24.1 0.2 compare_select_fusion
  24.3 226.8 %scatter_custom_fusion = s32[17]{0:T(128)S(1)} fusion(s32[32768]{0:T(1024)S(1)} %bitcast.23, s32[32768]{0:T(1024)S(1)} %broadcast.281, s32[]{:T(128)} %constant.16.clone.1), kind=kCustom, calls=%fused_computation.34 | custom fusion | flops 32768 | bytes 72 | tf_op jit(solution)/shard_map/scatter-add | solution.py:12
  251.1 0.1 copy.10
  251.3 0.1 reduce
  251.4 0.1 compare_select_fusion.3
  251.5 0.1 reshape.290
  251.6 11.2 %sort.17 = (s32[32768]{0:T(1024)}, s32[32768]{0:T(1024)S(1)}) sort(s32[32768]{0:T(1024)S(1)} %and_select_fusion.2, s32[32768]{0:T(1024)S(1)} %iota.14), dimensions={0}, to_apply=%region_0.1 | sort | flops 491520 | bytes 524288 | tf_op jit(solution)/shard_map/jit(argsort)/sort | solution.py:11
  262.8 43.1 %gather_fusion = s32[8320]{0:T(1024)S(1)} fusion(s32[32768]{0:T(1024)S(1)} %get-tuple-element.6, s32[9216]{0:T(1024)S(1)} %pad_clamp_fusion.2), kind=kCustom, calls=%fused_computation | custom fusion | bytes 99840 | tf_op jit(solution)/shard_map/gather | solution.py:15
  305.9 0.1 gather.15
  306.1 0.1 reshape.298
  306.2 0.1 reshape.306
  306.3 0.0 copy-done
  306.3 11.1 %all_gather.11 = f32[4096,8]{0,1:T(8,128)S(1)} all-gather(f32[512,8]{0,1:T(8,128)S(1)} %copy-done), channel_id=1, replica_groups=mesh['dp'=1,'tp'=2,'ep'=4] {'ep','tp'}, dimensions={0}, use_global_device_ids=true | all-gather | bytes 147456 | tf_op jit(solution)/shard_map/all_gather | solution.py:37
  317.4 0.6 copy.11
  318.0 1.0 reshape.286
  319.0 43.3 %gather_fusion.2 = f32[8320]{0:T(1024)S(1)} fusion(f32[32768]{0:T(1024)S(1)} %reshape.286, s32[9216]{0:T(1024)S(1)} %pad_clamp_fusion), kind=kCustom, calls=%fused_computation.2 | custom fusion | bytes 99840 | tf_op jit(solution)/shard_map/gather | solution.py:16
  362.3 0.1 reshape.305
  362.4 0.9 fusion.5
  363.3 0.1 fusion.4
  363.4 0.0 all-gather.2.cloned.1.call-done
  363.4 70.8 %gather_fusion.1 = bf16[8320,2048]{1,0:T(8,128)(2,1)} fusion(bf16[4096,2048]{1,0:T(8,128)(2,1)} %all-gather.2.cloned.1.call-done, s32[9216]{0:T(1024)S(1)} %pad_clamp_fusion.1), kind=kCustom, calls=%fused_computation.1 | custom fusion | bytes 68190720 | tf_op jit(solution)/shard_map/gather | solution.py:21
  434.2 32.2 %fusion.10 = f32[16,520,512]{2,1,0:T(8,128)} fusion(bf16[16,520,2048]{2,1,0:T(8,128)(2,1)} %bitcast.21, bf16[16,2048,512]{2,1,0:T(8,128)(2,1)} %param.9), kind=kOutput, calls=%fused_computation.40 | convolution fusion | flops 17448304640 | bytes 84672512 | tf_op jit(solution)/shard_map/ecd,edf->ecf/dot_general | solution.py:22
  466.5 66.3 %broadcast_multiply_fusion = f32[16,520,2048]{2,1,0:T(8,128)} fusion(f32[16,520]{1,0:T(8,128)S(1)} %fusion.4, bf16[16,512,2048]{2,1,0:T(8,128)(2,1)} %param.11, f32[16,520,512]{2,1,0:T(8,128)} %fusion.10, bf16[16,520,2048]{2,1,0:T(8,128)(2,1)} %bitcast.22, bf16[16,2048,512]{2,1,0:T(8,128)(2,1)} %param.10), kind=kOutput, calls=%fused_computation.5 | convolution fusion | flops 34939207680 | bytes 186417664 | tf_op jit(solution)/shard_map/ecf,efd->ecd/dot_general | solution.py:25
  532.8 121.3 %scatter_custom_fusion.1 = f32[4096,2048]{1,0:T(8,128)} fusion(s32[8320]{0:T(1024)} %fusion.5, f32[8320,2048]{1,0:T(8,128)} %bitcast.3, f32[]{:T(128)} %constant.13.clone.1), kind=kCustom, calls=%fused_computation.7 | custom fusion | flops 17039360 | bytes 33554944 | tf_op jit(solution)/shard_map/scatter-add | solution.py:27
  654.1 0.0 reduce-scatter.2.cloned.1.call-update
  654.2 196.4 %reduce-scatter.2.cloned.1.call-done = f32[512,2048]{1,0:T(8,128)} async-done(((f32[4096,2048]{1,0:T(8,128)}), f32[512,2048]{1,0:T(8,128)}) %reduce-scatter.2.cloned.1.call-update) | async-done | bytes 4194320 | tf_op jit(solution)/shard_map/reduce_scatter | solution.py:44
  850.5 3.8 convert_element_type.7
  (11 shorter events, 0.2 us)
Async XLA Ops:
  6.5 299.7 %copy-start = (f32[512,8]{0,1:T(8,128)S(1)}, f32[512,8]{0,1:T(8,128)}, u32[]{:S(2)}) copy-start(f32[512,8]{0,1:T(8,128)} %param.8) | copy-start | bytes 49156
  6.5 356.8 %all-gather.2.cloned.1.call-start = ((), (), s32[]{:S(2)}) async-start(), calls=%async_computation.1 | async-start | bytes 18874368 | tf_op jit(solution)/shard_map/all_gather | solution.py:35
  7.3 843.3 %reduce-scatter.2.cloned.1.call-start = ((), (), s32[]{:S(2)}) async-start(), calls=%async_computation.2 | async-start | bytes 37748736 | tf_op jit(solution)/shard_map/reduce_scatter | solution.py:44
Sparse Core Ops, SparseCore 0:
  9.2 86.8 all-gather.1
  654.3 196.1 reduce-scatter.1
where the time goes:
time: 865 us; the launch traced here: 861 us
  other arithmetic  365 us (42%)
  waiting for transfers between devices  197 us (23%)
  local copies, waits for them, and re-layouts  162 us (19%)
  matrix products  98.6 us (11%)
  blocking collectives  25.1 us (3%)
  between operations  13.8 us (2%)
    scatter-add x1, other arithmetic, _groups(): counts = jnp.zeros((n_exp + 1,), jnp.int32).at[key].add(1)[:n_exp]  227 us
    reduce_scatter x1, waiting for transfers between devices, body(): y = lax.psum_scatter(part, ('ep', 'tp'), scatter_dimension=0, tiled=True)  196 us
    scatter-add x1, other arithmetic, _experts(): jnp.zeros(x.shape, jnp.float32).at[tok.reshape(-1)].add(o.reshape(-1, d))  121 us
    gather x1, local copies, waits for them, and re-layouts, _experts(): xg = x[tok]  70.8 us
    dot_general x1, matrix products, _experts(): jnp.einsum('ecf,efd->ecd', h, w2, preferred_element_type=jnp.float32)  66.3 us
    gather x2, local copies, waits for them, and re-layouts, _groups(): g = jnp.where(slot[None, :] < counts[:, None], gate.reshape(-1)[pid], 0.0)  43.4 us
    gather x2, local copies, waits for them, and re-layouts, _groups(): pid = order[jnp.clip(starts[:, None] + slot[None, :], 0, flat.shape[0] - 1)]  43.2 us
    dot_general x1, matrix products, _experts(): a = jnp.einsum('ecd,edf->ecf', xg, w1, preferred_element_type=jnp.float32)  32.2 us
  transfers between devices with their start and end apart: 2, of which 1 were waited for; matrix products, arithmetic and copies ran while one was open for 38% of the time, Pallas kernels for 0%

commit v1 on v0

v1 whole, which is shorter than its diff:
```python
import functools

import jax
import jax.numpy as jnp
from jax import lax
from jax.experimental import pallas as pl
from jax.experimental.pallas import tpu as pltpu
from jax.sharding import PartitionSpec as P

PARTS = 2
BLOCK = 288
LO = 32


def _experts_kernel(slots, rows, cnt_ref, tok_ref, gate_ref, x_ref, w1_ref, w3_ref, w2_ref,
                    out_ref, acc_ref, xg_ref, o_ref, sem):
    e = pl.program_id(0)
    n = cnt_ref[e]
    chunks = x_ref.shape[1]
    half = chunks // 2

    @pl.when(e == 0)
    def _():
        def clear(i, _):
            b = pl.multiple_of(i * 8, 8)
            acc_ref[pl.ds(b, 8)] = jnp.zeros((8,) + acc_ref.shape[1:], jnp.float32)
            return 0
        lax.fori_loop(0, acc_ref.shape[0] // 8, clear, 0)

    def block(j, _):
        first = j * BLOCK
        base = e * slots + first
        left = jnp.minimum(n - first, BLOCK)

        def gather(i, _):
            b = pl.multiple_of(i * 16, 16)
            v = jnp.stack([x_ref[tok_ref[base + b + r]] for r in range(16)])
            v = jnp.swapaxes(v, 0, 1)
            for k in range(chunks):
                xg_ref[pl.ds(b, 16), k * 128:(k + 1) * 128] = v[k]
            return 0
        lax.fori_loop(0, (left + 15) // 16, gather, 0)

        xg = xg_ref[...]
        a = jnp.dot(xg, w1_ref[0], preferred_element_type=jnp.float32)
        b = jnp.dot(xg, w3_ref[0], preferred_element_type=jnp.float32)
        h = (jax.nn.silu(a) * b).astype(jnp.bfloat16)
        o_ref[...] = jnp.dot(h, w2_ref[0], preferred_element_type=jnp.float32)

        def scatter(i, _):
            b = pl.multiple_of(i * 8, 8)
            v = [jnp.swapaxes(jnp.stack([o_ref[pl.ds(b, 8), k * 128:(k + 1) * 128]
                                         for k in range(s * half, (s + 1) * half)]), 0, 1) for s in range(2)]
            for r in range(8):
                t = tok_ref[base + b + r]
                g = gate_ref[e * rows + t]
                t = jnp.where(b + r < left, t, rows)
                for s in range(2):
                    sl = slice(s * half, (s + 1) * half)
                    acc_ref[t, sl] = acc_ref[t, sl] + v[s][r] * g
            return 0
        lax.fori_loop(0, (left + 7) // 8, scatter, 0)
        return 0

    lax.fori_loop(0, (n + BLOCK - 1) // BLOCK, block, 0)

    @pl.when(e == pl.num_programs(0) - 1)
    def _():
        copy = pltpu.make_async_copy(acc_ref.at[pl.ds(0, rows)], out_ref, sem)
        copy.start()
        copy.wait()


def _experts(cnt, tok, ge, x3, w1, w3, w2):
    n_exp, d, f = w1.shape
    rows, chunks, lanes = x3.shape
    slots = tok.shape[1]
    once = pl.Buffered(1)
    return pl.pallas_call(
        functools.partial(_experts_kernel, slots, rows),
        grid_spec=pltpu.PrefetchScalarGridSpec(
            num_scalar_prefetch=3, grid=(n_exp,),
            in_specs=[pl.BlockSpec((rows, chunks, lanes), lambda e, *_: (0, 0, 0), pipeline_mode=once),
                      pl.BlockSpec((1, d, f), lambda e, *_: (e, 0, 0)),
                      pl.BlockSpec((1, d, f), lambda e, *_: (e, 0, 0)),
                      pl.BlockSpec((1, f, d), lambda e, *_: (e, 0, 0))],
            out_specs=pl.BlockSpec(memory_space=pl.ANY),
            scratch_shapes=[pltpu.VMEM((rows + 8, chunks, lanes), jnp.float32),
                            pltpu.VMEM((BLOCK, d), jnp.bfloat16),
                            pltpu.VMEM((BLOCK, d), jnp.float32),
                            pltpu.SemaphoreType.DMA]),
        out_shape=jax.ShapeDtypeStruct((rows, chunks, lanes), jnp.float32),
        compiler_params=pltpu.CompilerParams(vmem_limit_bytes=60 << 20),
        cost_estimate=pl.CostEstimate(flops=6 * n_exp * BLOCK * d * f, transcendentals=n_exp * BLOCK * f,
                                      bytes_accessed=6 * n_exp * d * f + 6 * rows * d),
        name='experts',
    )(cnt, tok.reshape(-1), ge.reshape(-1), x3, w1, w3, w2)


def _lists(idx_t, gate_t, lo, n_exp, slots):
    parts, _, rows = idx_t.shape
    bf, f32 = jnp.bfloat16, jnp.float32
    e = lo + jnp.arange(n_exp, dtype=jnp.int32)
    hit = idx_t[:, None] == e[None, :, None, None]
    mask = jnp.any(hit, axis=2)
    ge = jnp.sum(jnp.where(hit, gate_t[:, None], 0.0), axis=2)
    blk = mask.reshape(parts, n_exp, rows // 128, 128).astype(bf)
    i = jnp.arange(128)
    within = jnp.einsum('pent,ts->pens', blk, (i[:, None] < i[None, :]).astype(bf), preferred_element_type=f32)
    tot = jnp.sum(blk.astype(f32), axis=-1)
    m = jnp.arange(rows // 128)
    before = jnp.einsum('pen,nm->pem', tot.astype(bf), (m[:, None] < m[None, :]).astype(bf), preferred_element_type=f32)
    pos = (within + before[..., None]).reshape(parts, n_exp, rows).astype(jnp.int32)
    cnt = jnp.sum(tot, axis=-1).astype(jnp.int32)
    t = jnp.arange(rows, dtype=jnp.int32)
    hi = jnp.where(mask, pos // LO, -1)[:, :, None] == jnp.arange(slots // LO)[None, None, :, None]
    low = ((pos % LO)[:, :, None] == jnp.arange(LO)[None, None, :, None]).astype(bf)
    put = lambda v: jnp.einsum('peqt,pelt->peql', jnp.where(hi, v.astype(bf), 0), low, preferred_element_type=f32)
    tok = (put(t // 256) * 256 + put(t % 256)).astype(jnp.int32)
    return cnt, tok.reshape(parts, n_exp, slots), ge


def solution(mesh):
    rows_spec = P(('dp', 'ep', 'tp'), None)
    group = ('ep', 'tp')

    def body(x, idx, gate, w1, w3, w2):
        rows, d = x.shape
        n_exp, k = w1.shape[0], idx.shape[1]
        r = rows // PARTS
        x3 = x.reshape(rows, d // 128, 128)
        xa = [lax.all_gather(x3[p * r:(p + 1) * r], group, axis=0, tiled=True) for p in range(PARTS)]
        meta = jnp.concatenate([idx.astype(jnp.float32), gate], axis=1)
        meta = meta.reshape(PARTS, r, 2 * k).transpose(0, 2, 1)
        ma = lax.all_gather(meta, group, axis=2, tiled=True)
        lo = lax.axis_index('ep') * n_exp
        total = ma.shape[2]
        slots = BLOCK * (-(-min(520, total) // BLOCK))
        cnt, tok, ge = _lists(ma[:, :k].astype(jnp.int32), ma[:, k:], lo, n_exp, slots)
        outs = []
        for p in range(PARTS):
            part = _experts(cnt[p], tok[p], ge[p], xa[p], w1, w3, w2)
            outs.append(lax.psum_scatter(part, group, scatter_dimension=0, tiled=True))
        return jnp.concatenate([o.astype(jnp.bfloat16) for o in outs], axis=0).reshape(rows, d)

    return jax.shard_map(body, mesh=mesh,
                         in_specs=(rows_spec, rows_spec, rows_spec,
                                   P('ep', None, 'tp'), P('ep', None, 'tp'), P('ep', 'tp', None)),
                         out_specs=rows_spec, check_vma=False)
```

time: 865 us -> 368 us (0.43)
  other arithmetic: 365 us -> 5.74 us
  Pallas kernels: 0 us -> 154 us
  local copies, waits for them, and re-layouts: 162 us -> 9.52 us
  matrix products: 98.6 us -> 4.78 us
  waiting for transfers between devices: 197 us -> 162 us
    scatter-add x2 -> x0, other arithmetic: 348 us -> none  [the longest x1 227 us: _groups(): counts = jnp.zeros((n_exp + 1,), jnp.int32).at[key].add(1)[:n_exp]]
    gather x5 -> x0, local copies, waits for them, and re-layouts: 157 us -> none  [the longest x1 70.8 us: _experts(): xg = x[tok]]
    pallas_call x0 -> x2, Pallas kernels: none -> 154 us  [_experts(): pl.pallas_call(functools.partial(_experts_kernel, slots, rows), grid_spec...]
    dot_general x2 -> x4, matrix products: 98.6 us -> 4.78 us  [the longest x2 4.47 us: _lists(): jnp.einsum('peqt,pelt->peql', jnp.where(hi, v.astype(bf), 0), low, prefer...]
    reduce_scatter x1 -> x2, waiting for transfers between devices: 196 us -> 137 us  [body(): outs.append(lax.psum_scatter(part, group, scatter_dimension=0, tiled=True))]
    all_gather x1 -> x2, waiting for transfers between devices: 0.01 us -> 25.5 us  [body(): lax.all_gather(x3[p * r:(p + 1) * r], group, axis=0, tiled=True)]
    sort x1 -> x0, other arithmetic: 11.2 us -> none  [_groups(): order = jnp.argsort(key)]
    all_gather x2 -> x1, blocking collectives: 25.1 us -> 16.9 us  [body(): ma = lax.all_gather(meta, group, axis=2, tiled=True)]
  transfers between devices with their start and end apart: 2 -> 4, of which waited for: 1 -> 3; matrix products, arithmetic and copies ran while one was open for 38% -> 4% of each run, Pallas kernels for 0% -> 42%
where the time goes in v1:
time: 368 us; the launch traced here: 367 us
  waiting for transfers between devices  162 us (44%)
  Pallas kernels  154 us (42%)
  blocking collectives  16.9 us (5%)
  between operations  13.3 us (4%)
  local copies, waits for them, and re-layouts  9.52 us (3%)
  other arithmetic  5.74 us (2%)
  matrix products  4.78 us (1%)
    pallas_call x2, Pallas kernels, _experts(): pl.pallas_call(functools.partial(_experts_kernel, slots, rows), grid_spec...  154 us
    reduce_scatter x2, waiting for transfers between devices, body(): outs.append(lax.psum_scatter(part, group, scatter_dimension=0, tiled=True))  137 us
    all_gather x2, waiting for transfers between devices, body(): lax.all_gather(x3[p * r:(p + 1) * r], group, axis=0, tiled=True)  25.5 us
    all_gather x1, blocking collectives, body(): ma = lax.all_gather(meta, group, axis=2, tiled=True)  16.9 us
    unnamed x12, local copies, waits for them, and re-layouts  7.46 us
  transfers between devices with their start and end apart: 4, of which 3 were waited for; matrix products, arithmetic and copies ran while one was open for 4% of the time, Pallas kernels for 42%

profile of v1, /device:TPU:0, one launch (start us, length us, event | category | flops | bytes accessed | tf_op | source)
XLA Modules:
  0.0 367.4 jit_solution(13456340773537794972)
XLA Ops:
  6.5 0.0 all-gather.3.cloned.1.call-start
  6.5 1.7 slice_bitcast_fusion.1
  8.2 0.0 copy-start
  8.2 0.0 copy-start.1
  8.2 1.3 copy.20
  9.5 0.0 all-gather.3.cloned.1.call-update
  9.6 0.0 all-gather.5.cloned.1.call-start
  9.6 1.2 copy.22
  10.8 0.0 all-gather.5.cloned.1.call-update
  10.8 0.0 reduce-scatter.3.cloned.1.call-start
  10.9 0.0 copy-done
  10.9 0.0 copy-done.1
  10.9 16.9 %all_gather.9 = f32[2,16,2048]{2,1,0:T(8,128)S(1)} all-gather(f32[2,16,256]{2,1,0:T(8,128)S(1)} %bitcast.58), channel_id=1, replica_groups=mesh['dp'=1,'tp'=2,'ep'=4] {'ep','tp'}, dimensions={2}, use_global_device_ids=true | all-gather | bytes 294912 | tf_op jit(solution)/shard_map/all_gather | solution.py:135
  27.9 0.8 compare_reduce_fusion
  28.8 0.2 fusion.29
  28.9 0.1 fusion.42
  29.0 0.2 fusion.24
  29.3 0.2 fusion.25
  29.6 2.1 fusion
  31.7 2.3 fusion.21
  34.1 0.7 reshape_squeeze.12.tok_ref
  34.8 0.1 convert_reduce_fusion
  34.9 0.7 fusion.10
  35.7 0.7 copy.19
  36.4 0.6 slice_bitcast_fusion.5
  36.9 25.5 %all-gather.3.cloned.1.call-done.x_ref = bf16[2048,16,128]{2,1,0:T(8,128)(2,1)} async-done(((bf16[256,16,128]{2,1,0:T(8,128)(2,1)}), bf16[2048,16,128]{2,1,0:T(8,128)(2,1)}) %all-gather.3.cloned.1.call-update) | async-done | bytes 8388624 | tf_op jit(solution)/shard_map/all_gather | solution.py:132
  62.4 77.2 %experts.2 = f32[2048,16,128]{2,1,0:T(8,128)} custom-call(s32[16]{0:T(128)} %get-tuple-element.15.cnt_ref, s32[9216]{0:T(1024)} %reshape_squeeze.12.tok_ref, f32[32768]{0:T(1024)} %bitcast.56, bf16[2048,16,128]{2,1,0:T(8,128)(2,1)} %all-gather.3.cloned.1.call-done.x_ref, bf16[16,2048,512]{2,1,0:T(8,128)(2,1)} %w1_ref.3, bf16[16,2048,512]{2,1,0:T(8,128)(2,1)} %w3_ref.3, ...), custom_call_target="tpu_custom_call" | custom-call | flops 28991029248 | bytes 125829120 | tf_op jit(solution)/shard_map/experts/pallas_call | solution.py:79
  139.6 0.0 reduce-scatter.3.cloned.1.call-update
  139.6 0.2 reduce-scatter.5.cloned.1.call-start
  139.9 0.7 reshape_squeeze.14.tok_ref
  140.6 0.7 copy.21
  141.2 0.0 all-gather.5.cloned.1.call-done.x_ref
  141.3 77.2 %experts.3 = f32[2048,16,128]{2,1,0:T(8,128)} custom-call(s32[16]{0:T(128)} %get-tuple-element.16.cnt_ref, s32[9216]{0:T(1024)} %reshape_squeeze.14.tok_ref, f32[32768]{0:T(1024)} %bitcast.57, bf16[2048,16,128]{2,1,0:T(8,128)(2,1)} %all-gather.5.cloned.1.call-done.x_ref, bf16[16,2048,512]{2,1,0:T(8,128)(2,1)} %w1_ref.3, bf16[16,2048,512]{2,1,0:T(8,128)(2,1)} %w3_ref.3, ...), custom_call_target="tpu_custom_call" | custom-call | flops 28991029248 | bytes 125829120 | tf_op jit(solution)/shard_map/experts/pallas_call | solution.py:79
  218.4 0.0 reduce-scatter.5.cloned.1.call-update
  218.4 28.3 %reduce-scatter.3.cloned.1.call-done = f32[256,16,128]{2,1,0:T(8,128)} async-done(((f32[2048,16,128]{2,1,0:T(8,128)}), f32[256,16,128]{2,1,0:T(8,128)}) %reduce-scatter.3.cloned.1.call-update) | async-done | bytes 2097168 | tf_op jit(solution)/shard_map/reduce_scatter | solution.py:143
  246.7 1.7 convert_element_type.65
  248.5 108.6 %reduce-scatter.5.cloned.1.call-done = f32[256,16,128]{2,1,0:T(8,128)} async-done(((f32[2048,16,128]{2,1,0:T(8,128)}), f32[256,16,128]{2,1,0:T(8,128)}) %reduce-scatter.5.cloned.1.call-update) | async-done | bytes 2097168 | tf_op jit(solution)/shard_map/reduce_scatter | solution.py:143
  357.0 1.7 convert_element_type.66
  358.8 0.2 pad_maximum_fusion
  359.0 1.9 copy.26
  (12 shorter events, 0.2 us)
Async XLA Ops:
  6.5 55.9 %all-gather.3.cloned.1.call-start = ((), (), s32[]{:S(2)}) async-start(), calls=%async_computation.2 | async-start | bytes 9437184 | tf_op jit(solution)/shard_map/all_gather | solution.py:132
  8.2 2.7 copy-start
  8.2 2.7 copy-start.1
  9.6 131.7 %all-gather.5.cloned.1.call-start = ((), (), s32[]{:S(2)}) async-start(), calls=%async_computation.4 | async-start | bytes 9437184 | tf_op jit(solution)/shard_map/all_gather | solution.py:132
  10.8 235.9 %reduce-scatter.3.cloned.1.call-start = ((), (), s32[]{:S(2)}) async-start(), calls=%async_computation.3 | async-start | bytes 18874368 | tf_op jit(solution)/shard_map/reduce_scatter | solution.py:143
  139.6 217.4 %reduce-scatter.5.cloned.1.call-start = ((), (), s32[]{:S(2)}) async-start(), calls=%async_computation.5 | async-start | bytes 18874368 | tf_op jit(solution)/shard_map/reduce_scatter | solution.py:143
Sparse Core Ops, SparseCore 0:
  9.7 52.7 all-gather.2
  64.2 48.3 all-gather.4
  139.7 106.9 reduce-scatter.2
  250.1 106.9 reduce-scatter.4
